TPU v7x, 32 devices: a whole 2x2x4 slice. The times are simulated.
32 devices in a mesh: grid: 8 (over z, x), band: 4 (over y, core).
Axes of the slice: x: 2, y: 2, z: 4, core: 2. Of those that a mesh axis runs over, the one named last changes fastest.
Arguments:
- psi: bfloat16 [2048, 16, 512], P('band', 'grid'), may hold values from -6 to 6
- ritz_matrix: float32 [2048, 2048], P('band'), may hold values from -0.125 to 0.125
- potential: float32 [16, 512], P('grid'), may hold values from 0.5 to 10, as said below
Outputs:
- rotated: bfloat16 [2048, 16, 512], P('band', 'grid')
- search: bfloat16 [2048, 16, 512], P('band', 'grid')
Inputs may be any that keep to these rules, and one draw needn't show every extreme that they name: `potential`: positive everywhere.
All inputs are finite; a program needn't handle non-finite values.
Results may differ from a plain program's by a relative error of at most 0.0049.
Values may be sent and summed in bfloat16 or wider, within the bound.
A program may use at most 64 MiB of HBM per device.

v0:
```python
import jax
import jax.numpy as jnp
from jax import lax
from jax.sharding import PartitionSpec as P

NZ = 64


epsilon_mean = 1e-06


def with_halo(value, sides, width):
    for axis, dim in sides:
        count, length = (lax.axis_size(axis), value.shape[dim])
        up = [(i, (i + 1) % count) for i in range(count)]
        down = [(j, i) for i, j in up]
        last = lax.slice_in_dim(value, length - width, length, axis=dim)
        first = lax.slice_in_dim(value, 0, width, axis=dim)
        before = lax.ppermute(last, axis, up)
        after = lax.ppermute(first, axis, down)
        value = jnp.concatenate([before, value, after], axis=dim)
    return value


def apply_residual(padded, potential):
    center = padded[:, 1:-1].astype(jnp.float32)
    neighbours = padded[:, 2:].astype(jnp.float32) + padded[:, :-2].astype(jnp.float32)
    shaped = center.reshape(center.shape[0], center.shape[1], -1, NZ)
    across = (
        jnp.roll(shaped, 1, 2)
        + jnp.roll(shaped, -1, 2)
        + jnp.roll(shaped, 1, 3)
        + jnp.roll(shaped, -1, 3)
    )
    laplacian = neighbours + across.reshape(center.shape) - 6.0 * center
    resid = -0.5 * laplacian + potential[None] * center
    return (center, resid)


def shards(psi, ritz_matrix, potential):
    band_count = psi.shape[0]
    planes_dev = psi.shape[1]
    face_cells = psi.shape[2]
    piece = lax.all_gather(psi, "band", axis=0, tiled=True)
    flattened = piece.reshape(piece.shape[0], -1).astype(jnp.float32)
    folded = jnp.dot(ritz_matrix, flattened, precision=lax.Precision.HIGHEST)
    rotated = folded.reshape(band_count, planes_dev, face_cells).astype(jnp.bfloat16)
    padded = with_halo(rotated, (("grid", 1),), 1)
    center, resid = apply_residual(padded, potential)
    total_cells = planes_dev * face_cells * lax.axis_size("grid")
    cross_local = jnp.sum(center * resid, axis=(1, 2))
    self_local = jnp.sum(center * center, axis=(1, 2))
    resid_local = jnp.sum(resid * resid, axis=(1, 2))
    cross_sum, self_sum, resid_sum = lax.psum((cross_local, self_local, resid_local), "grid")
    m_cross = cross_sum / total_cells
    m_plain = self_sum / total_cells
    ratio = m_cross / (m_plain + epsilon_mean)
    direction = resid - ratio[:, None, None] * center
    m_dir = resid_sum / total_cells - 2.0 * ratio * m_cross + ratio * ratio * m_plain
    search = direction * lax.rsqrt(m_dir + epsilon_mean)[:, None, None]
    return (rotated, search.astype(jnp.bfloat16))


def solution(mesh):
    return jax.shard_map(
        shards,
        mesh=mesh,
        in_specs=(P("band", "grid", None), P("band", None), P("grid", None)),
        out_specs=(P("band", "grid", None), P("band", "grid", None)),
        check_vma=False,
    )
```

profile of v0, /device:TPU:0, one launch (start us, length us, event | category | flops | bytes accessed | tf_op | source)
XLA Modules:
  0.0 136.8 jit_solution(16779906986271277849)
XLA Ops:
  7.2 0.0 all-gather.2.cloned.1.call-start
  7.2 0.7 all-gather.2.cloned.1.call-update
  7.9 38.8 %all-gather.2.cloned.1.call-done = bf16[2048,2,512]{2,1,0:T(2,128)(2,1)} async-done(((bf16[512,2,512]{2,1,0:T(2,128)(2,1)}), bf16[2048,2,512]{2,1,0:T(2,128)(2,1)}) %all-gather.2.cloned.1.call-update) | async-done | bytes 4194320 | tf_op jit(solution)/shard_map/all_gather | solution.py:44
  46.7 11.2 %copy.11 = bf16[2048,2,512]{0,2,1:T(8,128)(2,1)} copy(bf16[2048,2,512]{2,1,0:T(2,128)(2,1)} %all-gather.2.cloned.1.call-done) | data formatting | bytes 8388608 | tf_op jit(solution)/shard_map/reshape | solution.py:45
  58.0 9.8 %fusion.13 = bf16[512,2,512]{0,2,1:T(8,128)(2,1)S(1)} fusion(bf16[2048,2,512]{0,2,1:T(8,128)(2,1)} %copy.11, f32[512,2048]{1,0:T(8,128)} %param.4), kind=kOutput, calls=%fused_computation.21 | convolution fusion | flops 12885426176 | bytes 9437184 | tf_op jit(solution)/shard_map/dot_general | solution.py:46
  67.8 2.5 %fusion.19 = (f32[512,2,8,63]{0,3,2,1:T(8,128)}, f32[512,2,8,63]{0,3,2,1:T(8,128)}) fusion(bf16[512,2,8,64]{0,3,2,1:T(8,128)(2,1)S(1)} %bitcast.26), kind=kLoop, calls=%fused_computation.27 | loop fusion | bytes 8257536 | tf_op jit(solution)/shard_map/jit(_roll_static)/slice | solution.py:33
  70.3 0.8 fusion.22
  71.2 1.0 fusion.18
  72.2 2.1 %copy.9 = bf16[512,2,512]{2,1,0:T(2,128)(2,1)} copy(bf16[512,2,512]{0,2,1:T(8,128)(2,1)S(1)} %fusion.13) | data formatting | bytes 2097152
  74.3 4.2 %collective-permute-start = (bf16[512,1,512]{0,2,1:T(8,128)(2,1)}, bf16[512,1,512]{0,2,1:T(8,128)(2,1)S(1)}, u32[]{:S(2)}, u32[]{:S(2)}) collective-permute-start(bf16[512,1,512]{0,2,1:T(8,128)(2,1)} %get-tuple-element.12), channel_id=1, source_target_pairs={{4,0},{8,4},{12,8},{16,12},{20,16},{24,20},{28,24},{0,28},{5,1},{9... | collective-permute-start | bytes 1572872 | tf_op jit(solution)/shard_map/ppermute | solution.py:20
  78.5 0.0 copy-start
  78.5 0.0 copy-start.1
  78.5 0.0 copy-start.4
  78.5 0.0 collective-permute-start.1
  78.5 0.5 fusion.21
  79.0 1.1 copy-done
  80.1 0.6 copy-done.1
  80.7 0.0 copy-done.4
  80.7 0.0 copy-start.5
  80.7 1.1 fusion.12
  81.8 18.0 %collective-permute-done = bf16[512,1,512]{0,2,1:T(8,128)(2,1)S(1)} collective-permute-done((bf16[512,1,512]{0,2,1:T(8,128)(2,1)}, bf16[512,1,512]{0,2,1:T(8,128)(2,1)S(1)}, u32[]{:S(2)}, u32[]{:S(2)}) %collective-permute-start) | collective-permute-done | bytes 524320 | tf_op jit(solution)/shard_map/ppermute | solution.py:20
  99.8 0.0 copy-start.2
  99.8 0.0 collective-permute-done.1
  99.8 0.0 copy-done.5
  99.8 0.0 copy-start.3
  99.8 1.3 fusion.6
  101.1 0.0 copy-done.2
  101.2 0.0 copy-done.3
  101.2 21.9 %all-reduce = (f32[512]{0:T(512)S(1)}, f32[512]{0:T(512)S(1)}, f32[512]{0:T(512)S(1)}) all-reduce(f32[512]{0:T(512)S(1)} %get-tuple-element.7, f32[512]{0:T(512)S(1)} %get-tuple-element.8, f32[512]{0:T(512)S(1)} %get-tuple-element.6), channel_id=1, replica_groups=mesh['grid'=8,'band'=4] {'grid'}, use_global_device_ids=true, to_apply=%region_5.6 | all-reduce | flops 1536 | bytes 12288 | tf_op jit(solution)/shard_map/psum | solution.py:54
  123.1 3.2 %fusion.10 = bf16[512,2,512]{0,2,1:T(8,128)(2,1)} fusion(bf16[512,2,512]{0,2,1:T(8,128)(2,1)S(1)} %fusion.13, f32[512]{0:T(512)S(1)} %get-tuple-element.23, f32[512]{0:T(512)S(1)} %get-tuple-element.22, f32[2,512]{1,0:T(2,128)S(1)} %copy-done.5, f32[512,2,8,64]{0,3,2,1:T(8,128)S(1)} %fusion.12, bf16[512,1,512]{0,2,1:T(8,128)(2,1)} %copy-done.3, ...), kind=kLoop, calls=%fused_computation.15 | loop fusion | flops 8388608 | bytes 5251072 | tf_op jit(solution)/shard_map/convert_element_type | solution.py:61
  126.3 3.7 %copy.10 = bf16[512,2,512]{2,1,0:T(2,128)(2,1)} copy(bf16[512,2,512]{0,2,1:T(8,128)(2,1)} %fusion.10) | data formatting | bytes 2097152
  (2 shorter events, 0.1 us)
Async XLA Ops:
  7.2 39.6 %all-gather.2.cloned.1.call-start = ((), (), s32[]{:S(2)}) async-start(), calls=%async_computation | async-start | bytes 5242880 | tf_op jit(solution)/shard_map/all_gather | solution.py:44
  74.3 25.5 %collective-permute-start = (bf16[512,1,512]{0,2,1:T(8,128)(2,1)}, bf16[512,1,512]{0,2,1:T(8,128)(2,1)S(1)}, u32[]{:S(2)}, u32[]{:S(2)}) collective-permute-start(bf16[512,1,512]{0,2,1:T(8,128)(2,1)} %get-tuple-element.12), channel_id=1, source_target_pairs={{4,0},{8,4},{12,8},{16,12},{20,16},{24,20},{28,24},{0,28},{5,1},{9... | collective-permute-start | bytes 1572872 | tf_op jit(solution)/shard_map/ppermute | solution.py:20
  78.5 1.6 %copy-start = (f32[512,2,8,63]{0,3,2,1:T(8,128)S(1)}, f32[512,2,8,63]{0,3,2,1:T(8,128)}, u32[]{:S(2)}) copy-start(f32[512,2,8,63]{0,3,2,1:T(8,128)} %get-tuple-element.14) | copy-start | bytes 6193156
  78.5 2.2 %copy-start.1 = (f32[512,2,8,63]{0,3,2,1:T(8,128)S(1)}, f32[512,2,8,63]{0,3,2,1:T(8,128)}, u32[]{:S(2)}) copy-start(f32[512,2,8,63]{0,3,2,1:T(8,128)} %get-tuple-element.15) | copy-start | bytes 6193156
  78.5 2.2 %copy-start.4 = (f32[512,2,1,64]{0,3,2,1:T(8,128)S(1)}, f32[512,2,1,64]{0,3,2,1:T(8,128)}, u32[]{:S(2)}) copy-start(f32[512,2,1,64]{0,3,2,1:T(8,128)} %get-tuple-element.21) | copy-start | bytes 786436
  78.5 21.3 %collective-permute-start.1 = (bf16[512,1,512]{0,2,1:T(8,128)(2,1)}, bf16[512,1,512]{0,2,1:T(8,128)(2,1)S(1)}, u32[]{:S(2)}, u32[]{:S(2)}) collective-permute-start(bf16[512,1,512]{0,2,1:T(8,128)(2,1)} %get-tuple-element.13), channel_id=1, source_target_pairs={{0,4},{4,8},{8,12},{12,16},{16,20},{20,24},{24,28},{28,0},{1,5},{5... | collective-permute-start | bytes 1572872 | tf_op jit(solution)/shard_map/ppermute | solution.py:19
  80.7 19.1 %copy-start.5 = (f32[2,512]{1,0:T(2,128)S(1)}, f32[2,512]{1,0:T(2,128)}, u32[]{:S(2)}) copy-start(f32[2,512]{1,0:T(2,128)} %param.5) | copy-start | bytes 12292
  99.8 1.4 copy-start.2
  99.8 1.4 copy-start.3
Sparse Core Ops, SparseCore 0:
  9.5 37.1 all-gather.1
where the time goes:
time: 137 us
  waiting for transfers between devices  57.5 us (42%)
  local copies, waits for them, and re-layouts  23.6 us (17%)
  blocking collectives  21.9 us (16%)
  between operations  14.1 us (10%)
  matrix products  9.83 us (7%)
  other arithmetic  5.62 us (4%)
  starting transfers between devices  4.28 us (3%)
    all_gather x1, waiting for transfers between devices, shards(): piece = lax.all_gather(psi, 'band', axis=0, tiled=True)  38.8 us
    psum x1, blocking collectives, shards(): lax.psum((cross_local, self_local, resid_local), 'grid')  21.9 us
    ppermute x1, waiting for transfers between devices, with_halo(): after = lax.ppermute(first, axis, down)  18 us
    reshape x1, local copies, waits for them, and re-layouts, shards(): flattened = piece.reshape(piece.shape[0], -1).astype(jnp.float32)  11.2 us
    dot_general x1, matrix products, shards(): folded = jnp.dot(ritz_matrix, flattened, precision=lax.Precision.HIGHEST)  9.83 us
    unnamed x14, local copies, waits for them, and re-layouts  7.49 us
    ppermute x1, starting transfers between devices, with_halo(): after = lax.ppermute(first, axis, down)  4.24 us
    convert_element_type x1, other arithmetic, shards(): return (rotated, search.astype(jnp.bfloat16))  3.19 us
  transfers between devices with their start and end apart: 3, of which 2 were waited for; matrix products, arithmetic and copies ran while one was open for 1% of the time, Pallas kernels for 0%

commit v1 on v0

v1 whole, which is shorter than its diff:
```python
import functools

import jax
import jax.numpy as jnp
from jax import lax
from jax.experimental import pallas as pl
from jax.experimental.pallas import tpu as pltpu
from jax.sharding import PartitionSpec as P

NZ = 64
CW = 128
EPS = 1e-06
MESH = pl.DeviceIdType.MESH


def fused(nb, ng, psi, ritz, pot, rot_out, search_out,
          ritz_f, ritz_s, buf, acc, stencil, rot, halo, resid, part, sums, gat,
          own_sem, ritz_sem, out_sem, far_send, far_recv, near_send, near_recv,
          fwd_send, fwd_recv, halo_send, halo_recv, red_send, red_recv):
    planes, bands, cells = rot.shape
    nq = cells // CW
    chunks = [(p, q) for q in range(nq) for p in range(planes)]
    nchip = nb // 2
    b = lax.axis_index("band")
    g = lax.axis_index("grid")
    chip, core = b // 2, b % 2
    sib = chip * 2 + (1 - core)
    up, down = lax.rem(g + 1, ng), lax.rem(g + ng - 1, ng)

    def far_of(o):
        return lax.rem(chip + o, nchip)

    barrier = pltpu.get_barrier_semaphore()
    for o in range(1, nchip):
        pl.semaphore_signal(barrier, inc=1, device_id={"band": far_of(o) * 2 + core}, device_id_type=MESH)
    pl.semaphore_signal(barrier, inc=1, device_id={"band": sib}, device_id_type=MESH)
    for o in range(1, ng):
        pl.semaphore_signal(barrier, inc=1, device_id={"grid": lax.rem(g + o, ng)}, device_id_type=MESH)

    ritz_copy = pltpu.make_async_copy(ritz, ritz_f, ritz_sem)
    own = []
    for c, (p, q) in enumerate(chunks):
        own.append(pltpu.make_async_copy(psi.at[p, :, pl.ds(q * CW, CW)], buf.at[c, b], own_sem.at[c]))
    for copy in own:
        copy.start()
    ritz_copy.start()

    pl.semaphore_wait(barrier, nchip - 1 + 1 + ng - 1)

    far = {}
    near = []
    for c, (p, q) in enumerate(chunks):
        for o in range(1, nchip):
            copy = pltpu.make_async_remote_copy(
                src_ref=psi.at[p, :, pl.ds(q * CW, CW)], dst_ref=buf.at[c, b],
                send_sem=far_send.at[c, o - 1], recv_sem=far_recv.at[c, o - 1],
                device_id={"band": far_of(o) * 2 + core}, device_id_type=MESH)
            copy.start()
            far[c, o] = copy
        copy = pltpu.make_async_remote_copy(
            src_ref=psi.at[p, :, pl.ds(q * CW, CW)], dst_ref=buf.at[c, b],
            send_sem=near_send.at[c], recv_sem=near_recv.at[c],
            device_id={"band": sib}, device_id_type=MESH)
        copy.start()
        near.append(copy)

    row = lax.broadcasted_iota(jnp.int32, (cells, cells), 0)
    col = lax.broadcasted_iota(jnp.int32, (cells, cells), 1)
    ny = cells // NZ

    def hits(dy, dz):
        y = lax.rem(col // NZ + dy + ny, ny)
        z = lax.rem(lax.rem(col, NZ) + dz + NZ, NZ)
        return (row == y * NZ + z).astype(jnp.float32)

    mat = -6.0 * (row == col).astype(jnp.float32)
    for dy, dz in ((1, 0), (-1, 0), (0, 1), (0, -1)):
        mat = mat + hits(dy, dz)
    stencil[...] = mat.astype(jnp.bfloat16)

    ritz_copy.wait()
    rows = min(bands, 32)

    def split(i, carry):
        at = pl.ds(pl.multiple_of(i * rows, rows), rows)
        whole = ritz_f[at, :]
        hi = whole.astype(jnp.bfloat16)
        rest = whole - hi.astype(jnp.float32)
        mid = rest.astype(jnp.bfloat16)
        ritz_s[0, at, :] = hi
        ritz_s[1, at, :] = mid
        ritz_s[2, at, :] = (rest - mid.astype(jnp.float32)).astype(jnp.bfloat16)
        return carry

    lax.fori_loop(0, bands // rows, split, 0)

    def product(block, first, width):
        at = pl.ds(pl.multiple_of(first * bands, width), width)
        total = jnp.dot(ritz_s[0, :, at], block, preferred_element_type=jnp.float32)
        total += jnp.dot(ritz_s[1, :, at], block, preferred_element_type=jnp.float32)
        total += jnp.dot(ritz_s[2, :, at], block, preferred_element_type=jnp.float32)
        return total

    pair = 2 * bands
    for c in range(len(chunks)):
        own[c].wait()
        near[c].wait_recv()
        acc[c] = product(buf[c, pl.ds(chip * 2, 2)].reshape(pair, CW), chip * 2, pair)

    halos = []
    for c, (p, q) in enumerate(chunks):
        forwards = []
        for o in range(1, nchip):
            src = far_of(nchip - o) * 2 + core
            far[c, o].wait_recv()
            copy = pltpu.make_async_remote_copy(
                src_ref=buf.at[c, src], dst_ref=buf.at[c, src],
                send_sem=fwd_send.at[c, o - 1], recv_sem=fwd_recv.at[c, o - 1],
                device_id={"band": sib}, device_id_type=MESH)
            copy.start()
            forwards.append(copy)
        for o in range(1, nchip):
            forwards[o - 1].wait_recv()
            there = far_of(nchip - o) * 2
            acc[c] += product(buf[c, pl.ds(there, 2)].reshape(pair, CW), there, pair)
        at = pl.ds(q * CW, CW)
        rot[p, :, at] = acc[c].astype(jnp.bfloat16)
        for side, edge, to in ((0, planes - 1, up), (1, 0, down)):
            if p == edge:
                copy = pltpu.make_async_remote_copy(
                    src_ref=rot.at[p, :, at], dst_ref=halo.at[side, q],
                    send_sem=halo_send.at[side, q], recv_sem=halo_recv.at[side, q],
                    device_id={"grid": to}, device_id_type=MESH)
                copy.start()
                halos.append((side, q, copy))
        for copy in forwards:
            copy.wait_send()

    rot_copy = pltpu.make_async_copy(rot, rot_out, out_sem)
    rot_copy.start()

    vr = min(bands, 64)
    for p in range(planes):
        def local(i, carry):
            at = pl.ds(pl.multiple_of(i * vr, vr), vr)
            center = rot[p, at, :]
            lap = jnp.dot(center, stencil[...], preferred_element_type=jnp.float32)
            for other in (p - 1, p + 1):
                if 0 <= other < planes:
                    lap += rot[other, at, :].astype(jnp.float32)
            resid[p, at, :] = -0.5 * lap + pot[pl.ds(p, 1), :] * center.astype(jnp.float32)
            return carry

        lax.fori_loop(0, bands // vr, local, 0)

    part[...] = jnp.zeros_like(part)

    def gather_sums(p, q):
        def body(i, carry):
            at = pl.ds(pl.multiple_of(i * vr, vr), vr)
            lanes = pl.ds(q * CW, CW)
            center = rot[p, at, lanes].astype(jnp.float32)
            value = resid[p, at, lanes]
            if p == 0:
                value -= 0.5 * halo[0, q, at, :].astype(jnp.float32)
            if p == planes - 1:
                value -= 0.5 * halo[1, q, at, :].astype(jnp.float32)
            resid[p, at, lanes] = value
            part[0, at, :] += center * value
            part[1, at, :] += center * center
            part[2, at, :] += value * value
            return carry

        lax.fori_loop(0, bands // vr, body, 0)

    for q in range(nq):
        for side, hq, copy in halos:
            if hq == q:
                copy.wait_recv()
        for p in range(planes):
            gather_sums(p, q)

    for k in range(3):
        sums[pl.ds(k, 1), :] = jnp.sum(part[k].T, axis=0, keepdims=True)
    sums[pl.ds(3, 1), :] = jnp.zeros((1, bands), jnp.float32)

    reds = []
    for o in range(1, ng):
        copy = pltpu.make_async_remote_copy(
            src_ref=sums, dst_ref=gat.at[o - 1],
            send_sem=red_send.at[o - 1], recv_sem=red_recv.at[o - 1],
            device_id={"grid": lax.rem(g + o, ng)}, device_id_type=MESH)
        copy.start()
        reds.append(copy)
    total = sums[...]
    for o in range(1, ng):
        reds[o - 1].wait_recv()
        total = total + gat[o - 1]

    count = float(planes * cells * ng)
    m_cross = total[0:1] / count
    m_plain = total[1:2] / count
    ratio = m_cross / (m_plain + EPS)
    m_dir = total[2:3] / count - 2.0 * ratio * m_cross + ratio * ratio * m_plain
    scale = lax.rsqrt(m_dir + EPS)
    part[0] = jnp.broadcast_to(ratio, (CW, bands)).T
    part[1] = jnp.broadcast_to(scale, (CW, bands)).T

    for p in range(planes):
        def last(i, carry):
            at = pl.ds(pl.multiple_of(i * vr, vr), vr)
            for q in range(nq):
                lanes = pl.ds(q * CW, CW)
                direction = resid[p, at, lanes] - part[0, at, :] * rot[p, at, lanes].astype(jnp.float32)
                search_out[p, at, lanes] = (direction * part[1, at, :]).astype(jnp.bfloat16)
            return carry

        lax.fori_loop(0, bands // vr, last, 0)

    rot_copy.wait()
    for copy in far.values():
        copy.wait_send()
    for copy in near:
        copy.wait_send()
    for _, _, copy in halos:
        copy.wait_send()
    for copy in reds:
        copy.wait_send()


def shards(nb, ng, psi, ritz_matrix, potential):
    bands, planes, cells = psi.shape
    total = ritz_matrix.shape[1]
    nq = cells // CW
    nch = nq * planes
    far = max(nb // 2 - 1, 1)
    dma = pltpu.SemaphoreType.DMA
    rot, search = pl.pallas_call(
        functools.partial(fused, nb, ng),
        out_shape=[jax.ShapeDtypeStruct((planes, bands, cells), jnp.bfloat16)] * 2,
        in_specs=[pl.BlockSpec(memory_space=pl.ANY), pl.BlockSpec(memory_space=pl.ANY),
                  pl.BlockSpec(memory_space=pltpu.VMEM)],
        out_specs=[pl.BlockSpec(memory_space=pl.ANY), pl.BlockSpec(memory_space=pltpu.VMEM)],
        scratch_shapes=[
            pltpu.VMEM((bands, total), jnp.float32),
            pltpu.VMEM((3, bands, total), jnp.bfloat16),
            pltpu.VMEM((nch, nb, bands, CW), jnp.bfloat16),
            pltpu.VMEM((nch, bands, CW), jnp.float32),
            pltpu.VMEM((cells, cells), jnp.bfloat16),
            pltpu.VMEM((planes, bands, cells), jnp.bfloat16),
            pltpu.VMEM((2, nq, bands, CW), jnp.bfloat16),
            pltpu.VMEM((planes, bands, cells), jnp.float32),
            pltpu.VMEM((3, bands, CW), jnp.float32),
            pltpu.VMEM((4, bands), jnp.float32),
            pltpu.VMEM((ng - 1, 4, bands), jnp.float32),
            dma((nch,)), dma, dma,
            dma((nch, far)), dma((nch, far)), dma((nch,)), dma((nch,)),
            dma((nch, far)), dma((nch, far)), dma((2, nq)), dma((2, nq)),
            dma((ng - 1,)), dma((ng - 1,)),
        ],
        compiler_params=pltpu.CompilerParams(
            collective_id=0, has_side_effects=True, vmem_limit_bytes=56 * 1024 * 1024),
        name="ritz_residual",
    )(psi.transpose(1, 0, 2), ritz_matrix, potential)
    return rot.transpose(1, 0, 2), search.transpose(1, 0, 2)


def solution(mesh):
    nb, ng = mesh.shape["band"], mesh.shape["grid"]
    return jax.shard_map(
        functools.partial(shards, nb, ng),
        mesh=mesh,
        in_specs=(P("band", "grid", None), P("band", None), P("grid", None)),
        out_specs=(P("band", "grid", None), P("band", "grid", None)),
        check_vma=False,
    )
```

time: 137 us -> 68 us (0.50)
  Pallas kernels: 0 us -> 58.2 us
  waiting for transfers between devices: 57.5 us -> 0 us
  blocking collectives: 21.9 us -> 0 us
  local copies, waits for them, and re-layouts: 23.6 us -> 8.91 us
  between operations: 14.1 us -> 0.64 us
  matrix products: 9.83 us -> 0 us
  other arithmetic: 5.62 us -> 0 us
  starting transfers between devices: 4.28 us -> 0 us
    pallas_call x0 -> x1, Pallas kernels: none -> 58.2 us  [shards(): pl.pallas_call(functools.partial(fused, nb, ng), out_shape=[jax.ShapeDtyp...]
    all_gather x1 -> x0, waiting for transfers between devices: 38.8 us -> none  [shards(): piece = lax.all_gather(psi, 'band', axis=0, tiled=True)]
    psum x1 -> x0, blocking collectives: 21.9 us -> none  [shards(): lax.psum((cross_local, self_local, resid_local), 'grid')]
    ppermute x2 -> x0, waiting for transfers between devices: 18 us -> none  [the longest x1 18 us: with_halo(): after = lax.ppermute(first, axis, down)]
    reshape x1 -> x0, local copies, waits for them, and re-layouts: 11.2 us -> none  [shards(): flattened = piece.reshape(piece.shape[0], -1).astype(jnp.float32)]
    dot_general x1 -> x0, matrix products: 9.83 us -> none  [shards(): folded = jnp.dot(ritz_matrix, flattened, precision=lax.Precision.HIGHEST)]
    slice x5 -> x0, local copies, waits for them, and re-layouts: 4.87 us -> none  [the longest x2 2.57 us: apply_residual(): jnp.roll(shaped, -1, 3)]
    ppermute x2 -> x0, starting transfers between devices: 4.24 us -> none  [the longest x1 4.24 us: with_halo(): after = lax.ppermute(first, axis, down)]
  transfers between devices with their start and end apart: 3 -> 0, of which waited for: 2 -> 0; matrix products, arithmetic and copies ran while one was open for 1% -> 0% of each run, Pallas kernels for 0% -> 0%
where the time goes in v1:
time: 68 us; the launch traced here: 67.8 us
  Pallas kernels  58.2 us (86%)
  local copies, waits for them, and re-layouts  8.91 us (13%)
    pallas_call x1, Pallas kernels, shards(): pl.pallas_call(functools.partial(fused, nb, ng), out_shape=[jax.ShapeDtyp...  58.2 us
    unnamed x3, local copies, waits for them, and re-layouts  8.91 us

profile of v1, /device:TPU:0, one launch (start us, length us, event | category | flops | bytes accessed | tf_op | source)
XLA Modules:
  0.0 67.8 jit_solution(15378686309328603344)
XLA Ops:
  0.6 2.4 %copy.9 = bf16[512,2,512]{2,0,1:T(8,128)(2,1)} copy(bf16[512,2,512]{2,1,0:T(2,128)(2,1)} %param.3) | data formatting | bytes 2097152 | tf_op args[0]
  3.0 58.2 %ritz_residual.1 = (bf16[2,512,512]{2,1,0:T(8,128)(2,1)}, bf16[2,512,512]{2,1,0:T(8,128)(2,1)}) custom-call(bf16[2,512,512]{2,1,0:T(8,128)(2,1)} %bitcast.5, f32[512,2048]{1,0:T(8,128)} %ritz.1, f32[2,512]{1,0:T(2,128)} %pot.1), custom_call_target="tpu_custom_call" | custom-call | tf_op jit(solution)/shard_map/ritz_residual/pallas_call | solution.py:238
  61.2 3.3 %copy.6 = bf16[512,2,512]{2,1,0:T(2,128)(2,1)} copy(bf16[512,2,512]{2,0,1:T(8,128)(2,1)} %bitcast.7) | data formatting | bytes 2097152
  64.5 3.3 %copy.7 = bf16[512,2,512]{2,1,0:T(2,128)(2,1)} copy(bf16[512,2,512]{2,0,1:T(8,128)(2,1)} %bitcast.6) | data formatting | bytes 2097152

commit v2 on v1

--- a/solution.py
+++ b/solution.py
@@ -14,7 +14,7 @@
 
 
 def fused(nb, ng, psi, ritz, pot, rot_out, search_out,
-          ritz_f, ritz_s, buf, acc, stencil, rot, halo, resid, part, sums, gat,
+          raw, ritz_f, ritz_s, buf, acc, stencil, rot, halo, resid, part, sums, gat,
           own_sem, ritz_sem, out_sem, far_send, far_recv, near_send, near_recv,
           fwd_send, fwd_recv, halo_send, halo_recv, red_send, red_recv):
     planes, bands, cells = rot.shape
@@ -37,46 +37,37 @@
     for o in range(1, ng):
         pl.semaphore_signal(barrier, inc=1, device_id={"grid": lax.rem(g + o, ng)}, device_id_type=MESH)
 
+    raws = []
+    for q in range(nq):
+        raws.append(pltpu.make_async_copy(psi.at[:, :, pl.ds(q * CW, CW)], raw.at[q], own_sem.at[q]))
+        raws[q].start()
     ritz_copy = pltpu.make_async_copy(ritz, ritz_f, ritz_sem)
-    own = []
-    for c, (p, q) in enumerate(chunks):
-        own.append(pltpu.make_async_copy(psi.at[p, :, pl.ds(q * CW, CW)], buf.at[c, b], own_sem.at[c]))
-    for copy in own:
-        copy.start()
     ritz_copy.start()
+    for q in range(nq):
+        raws[q].wait()
+        for p in range(planes):
+            buf[q, b, :, pl.ds(p * CW, CW)] = raw[q, :, p, :]
 
     pl.semaphore_wait(barrier, nchip - 1 + 1 + ng - 1)
 
     far = {}
     near = []
     for c, (p, q) in enumerate(chunks):
+        mine = buf.at[q, b, :, pl.ds(p * CW, CW)]
         for o in range(1, nchip):
             copy = pltpu.make_async_remote_copy(
-                src_ref=psi.at[p, :, pl.ds(q * CW, CW)], dst_ref=buf.at[c, b],
+                src_ref=mine, dst_ref=mine,
                 send_sem=far_send.at[c, o - 1], recv_sem=far_recv.at[c, o - 1],
                 device_id={"band": far_of(o) * 2 + core}, device_id_type=MESH)
             copy.start()
             far[c, o] = copy
+    for q in range(nq):
         copy = pltpu.make_async_remote_copy(
-            src_ref=psi.at[p, :, pl.ds(q * CW, CW)], dst_ref=buf.at[c, b],
-            send_sem=near_send.at[c], recv_sem=near_recv.at[c],
+            src_ref=buf.at[q, b], dst_ref=buf.at[q, b],
+            send_sem=near_send.at[q], recv_sem=near_recv.at[q],
             device_id={"band": sib}, device_id_type=MESH)
         copy.start()
         near.append(copy)
-
-    row = lax.broadcasted_iota(jnp.int32, (cells, cells), 0)
-    col = lax.broadcasted_iota(jnp.int32, (cells, cells), 1)
-    ny = cells // NZ
-
-    def hits(dy, dz):
-        y = lax.rem(col // NZ + dy + ny, ny)
-        z = lax.rem(lax.rem(col, NZ) + dz + NZ, NZ)
-        return (row == y * NZ + z).astype(jnp.float32)
-
-    mat = -6.0 * (row == col).astype(jnp.float32)
-    for dy, dz in ((1, 0), (-1, 0), (0, 1), (0, -1)):
-        mat = mat + hits(dy, dz)
-    stencil[...] = mat.astype(jnp.bfloat16)
 
     ritz_copy.wait()
     rows = min(bands, 32)
@@ -101,40 +92,66 @@
         total += jnp.dot(ritz_s[2, :, at], block, preferred_element_type=jnp.float32)
         return total
 
+    ny = cells // NZ
+
+    def build(i, carry):
+        at = pl.ds(pl.multiple_of(i * 64, 64), 64)
+        row = lax.broadcasted_iota(jnp.int32, (64, cells), 0) + i * 64
+        col = lax.broadcasted_iota(jnp.int32, (64, cells), 1)
+        dy = lax.rem(row // NZ - col // NZ + ny, ny)
+        dz = lax.rem(lax.rem(row, NZ) - lax.rem(col, NZ) + NZ, NZ)
+
+        def one(test):
+            return jnp.where(test, 1.0, 0.0)
+
+        mat = jnp.where(dz == 0, one(dy == 1) + one(dy == ny - 1), 0.0)
+        mat += jnp.where(dy == 0, one(dz == 1) + one(dz == NZ - 1), 0.0)
+        mat -= 6.0 * one(row == col)
+        stencil[at, :] = mat.astype(jnp.bfloat16)
+        return carry
+
     pair = 2 * bands
-    for c in range(len(chunks)):
-        own[c].wait()
-        near[c].wait_recv()
-        acc[c] = product(buf[c, pl.ds(chip * 2, 2)].reshape(pair, CW), chip * 2, pair)
-
+    wide = pair % 128 == 0 and bands % 128 != 0
     halos = []
-    for c, (p, q) in enumerate(chunks):
-        forwards = []
-        for o in range(1, nchip):
-            src = far_of(nchip - o) * 2 + core
-            far[c, o].wait_recv()
-            copy = pltpu.make_async_remote_copy(
-                src_ref=buf.at[c, src], dst_ref=buf.at[c, src],
-                send_sem=fwd_send.at[c, o - 1], recv_sem=fwd_recv.at[c, o - 1],
-                device_id={"band": sib}, device_id_type=MESH)
-            copy.start()
-            forwards.append(copy)
-        for o in range(1, nchip):
-            forwards[o - 1].wait_recv()
-            there = far_of(nchip - o) * 2
-            acc[c] += product(buf[c, pl.ds(there, 2)].reshape(pair, CW), there, pair)
-        at = pl.ds(q * CW, CW)
-        rot[p, :, at] = acc[c].astype(jnp.bfloat16)
-        for side, edge, to in ((0, planes - 1, up), (1, 0, down)):
-            if p == edge:
+    for q in range(nq):
+        near[q].wait_recv()
+        acc[...] = product(buf[q, pl.ds(chip * 2, 2)].reshape(pair, planes * CW), chip * 2, pair)
+        if q == 0:
+            lax.fori_loop(0, cells // 64, build, 0)
+        for p in range(planes):
+            c = q * planes + p
+            lanes = pl.ds(p * CW, CW)
+            forwards = []
+            for o in range(1, nchip):
+                src = far_of(nchip - o) * 2 + core
+                far[c, o].wait_recv()
                 copy = pltpu.make_async_remote_copy(
-                    src_ref=rot.at[p, :, at], dst_ref=halo.at[side, q],
-                    send_sem=halo_send.at[side, q], recv_sem=halo_recv.at[side, q],
-                    device_id={"grid": to}, device_id_type=MESH)
+                    src_ref=buf.at[q, src, :, lanes], dst_ref=buf.at[q, src, :, lanes],
+                    send_sem=fwd_send.at[c, o - 1], recv_sem=fwd_recv.at[c, o - 1],
+                    device_id={"band": sib}, device_id_type=MESH)
                 copy.start()
-                halos.append((side, q, copy))
-        for copy in forwards:
-            copy.wait_send()
+                forwards.append(copy)
+            for o in range(1, nchip):
+                there = far_of(nchip - o) * 2
+                if wide:
+                    forwards[o - 1].wait_recv()
+                    acc[:, lanes] += product(buf[q, pl.ds(there, 2), :, lanes].reshape(pair, CW), there, pair)
+                else:
+                    acc[:, lanes] += product(buf[q, there + core, :, lanes], there + core, bands)
+                    forwards[o - 1].wait_recv()
+                    acc[:, lanes] += product(buf[q, there + 1 - core, :, lanes], there + 1 - core, bands)
+            at = pl.ds(q * CW, CW)
+            rot[p, :, at] = acc[:, lanes].astype(jnp.bfloat16)
+            for side, edge, to in ((0, planes - 1, up), (1, 0, down)):
+                if p == edge:
+                    copy = pltpu.make_async_remote_copy(
+                        src_ref=rot.at[p, :, at], dst_ref=halo.at[side, q],
+                        send_sem=halo_send.at[side, q], recv_sem=halo_recv.at[side, q],
+                        device_id={"grid": to}, device_id_type=MESH)
+                    copy.start()
+                    halos.append((side, q, copy))
+            for copy in forwards:
+                copy.wait_send()
 
     rot_copy = pltpu.make_async_copy(rot, rot_out, out_sem)
     rot_copy.start()
@@ -228,6 +245,12 @@
         copy.wait_send()
 
 
+def weave(rot, search, rot_out, search_out):
+    for p in range(rot.shape[0]):
+        rot_out[:, p, :] = rot[p]
+        search_out[:, p, :] = search[p]
+
+
 def shards(nb, ng, psi, ritz_matrix, potential):
     bands, planes, cells = psi.shape
     total = ritz_matrix.shape[1]
@@ -242,10 +265,11 @@
                   pl.BlockSpec(memory_space=pltpu.VMEM)],
         out_specs=[pl.BlockSpec(memory_space=pl.ANY), pl.BlockSpec(memory_space=pltpu.VMEM)],
         scratch_shapes=[
+            pltpu.VMEM((nq, bands, planes, CW), jnp.bfloat16),
             pltpu.VMEM((bands, total), jnp.float32),
             pltpu.VMEM((3, bands, total), jnp.bfloat16),
-            pltpu.VMEM((nch, nb, bands, CW), jnp.bfloat16),
-            pltpu.VMEM((nch, bands, CW), jnp.float32),
+            pltpu.VMEM((nq, nb, bands, planes * CW), jnp.bfloat16),
+            pltpu.VMEM((bands, planes * CW), jnp.float32),
             pltpu.VMEM((cells, cells), jnp.bfloat16),
             pltpu.VMEM((planes, bands, cells), jnp.bfloat16),
             pltpu.VMEM((2, nq, bands, CW), jnp.bfloat16),
@@ -253,16 +277,26 @@
             pltpu.VMEM((3, bands, CW), jnp.float32),
             pltpu.VMEM((4, bands), jnp.float32),
             pltpu.VMEM((ng - 1, 4, bands), jnp.float32),
-            dma((nch,)), dma, dma,
-            dma((nch, far)), dma((nch, far)), dma((nch,)), dma((nch,)),
+            dma((nq,)), dma, dma,
+            dma((nch, far)), dma((nch, far)), dma((nq,)), dma((nq,)),
             dma((nch, far)), dma((nch, far)), dma((2, nq)), dma((2, nq)),
             dma((ng - 1,)), dma((ng - 1,)),
         ],
         compiler_params=pltpu.CompilerParams(
             collective_id=0, has_side_effects=True, vmem_limit_bytes=56 * 1024 * 1024),
         name="ritz_residual",
-    )(psi.transpose(1, 0, 2), ritz_matrix, potential)
-    return rot.transpose(1, 0, 2), search.transpose(1, 0, 2)
+    )(psi, ritz_matrix, potential)
+    step = min(bands, 128)
+    inner = pl.BlockSpec((planes, step, cells), lambda i: (0, i, 0))
+    outer = pl.BlockSpec((step, planes, cells), lambda i: (i, 0, 0))
+    return pl.pallas_call(
+        weave,
+        grid=(bands // step,),
+        out_shape=[jax.ShapeDtypeStruct((bands, planes, cells), jnp.bfloat16)] * 2,
+        in_specs=[inner] * 2,
+        out_specs=[outer] * 2,
+        name="weave",
+    )(rot, search)
 
 
 def solution(mesh):

time: 68 us -> 54.2 us (0.80)
  local copies, waits for them, and re-layouts: 8.91 us -> 0 us
  Pallas kernels: 58.2 us -> 53.4 us
    pallas_call x1, Pallas kernels: 58.2 us -> 49 us  [shards(): pl.pallas_call(functools.partial(fused, nb, ng), out_shape=[jax.ShapeDtyp...]
    unnamed x3 -> x0, local copies, waits for them, and re-layouts: 8.91 us -> none
    pallas_call x0 -> x1, Pallas kernels: none -> 4.39 us  [shards(): pl.pallas_call(weave, grid=(bands // step,), out_shape=[jax.ShapeDtypeStr...]
where the time goes in v2:
time: 54.2 us; the launch traced here: 54 us
  Pallas kernels  53.4 us (99%)
  between operations  0.64 us (1%)
    pallas_call x1, Pallas kernels, shards(): pl.pallas_call(functools.partial(fused, nb, ng), out_shape=[jax.ShapeDtyp...  49 us
    pallas_call x1, Pallas kernels, shards(): pl.pallas_call(weave, grid=(bands // step,), out_shape=[jax.ShapeDtypeStr...  4.39 us

profile of v2, /device:TPU:0, one launch (start us, length us, event | category | flops | bytes accessed | tf_op | source)
XLA Modules:
  0.0 54.0 jit_solution(7493026338614467757)
XLA Ops:
  0.6 49.0 %ritz_residual.1 = (bf16[2,512,512]{2,1,0:T(8,128)(2,1)}, bf16[2,512,512]{2,1,0:T(8,128)(2,1)}) custom-call(bf16[512,2,512]{2,1,0:T(2,128)(2,1)} %psi.1, f32[512,2048]{1,0:T(8,128)} %ritz.1, f32[2,512]{1,0:T(2,128)} %pot.1), custom_call_target="tpu_custom_call" | custom-call | tf_op jit(solution)/shard_map/ritz_residual/pallas_call | solution.py:261
  49.6 4.4 %weave.1 = (bf16[512,2,512]{2,1,0:T(2,128)(2,1)}, bf16[512,2,512]{2,1,0:T(2,128)(2,1)}) custom-call(bf16[2,512,512]{2,1,0:T(8,128)(2,1)} %get-tuple-element.4.rot, bf16[2,512,512]{2,1,0:T(8,128)(2,1)} %get-tuple-element.5.search), custom_call_target="tpu_custom_call" | custom-call | tf_op jit(solution)/shard_map/weave/pallas_call | solution.py:292
